TPU v7x, 32 devices: a whole 2x2x4 slice. The times are simulated.
32 devices in a mesh: srv: 16 (over z, y, x), grp: 2 (over core).
Axes of the slice: x: 2, y: 2, z: 4, core: 2. Of those that a mesh axis runs over, the one named last changes fastest.
Arguments:
- basis_modes: float32 [64, 64, 3072], P(None, ('srv', 'grp')), may hold values from -10 to 10
- weights: float32 [64], replicated, may hold values from 0.5 to 4
- snapshots: float32 [16, 64, 3072], P(None, 'srv', 'grp'), may hold values from -10 to 10
Outputs:
- new_modes: float32 [80, 64, 3072], P(None, ('srv', 'grp'))
- factor: float32 [80, 80], replicated
All inputs are finite; a program needn't handle non-finite values.
Results may differ from a plain program's by a relative error of at most 0.00009.
Values sent between devices are 32-bit elements; how exact they have to be, the bound alone decides.
No kernel may reach another device: no remote copies, remote signals or barrier semaphores. Data moves between devices by JAX's collectives and lax.ppermute only.
A program may use at most 64 MiB of HBM per device.

v0:
```python
import jax
import jax.numpy as jnp
from jax import lax
from jax.sharding import PartitionSpec as P

MODES = 64
SNAPS = 16


def merged_factor(local_gram):
    return jnp.linalg.cholesky(lax.psum(local_gram, ("srv", "grp")))


def per_device(basis_modes, weights, snapshots):
    width = MODES + SNAPS
    total_cells = (
        basis_modes.shape[1] * basis_modes.shape[2] * lax.axis_size("srv") * lax.axis_size("grp")
    )
    scaled = basis_modes * weights[:, None, None]
    arrived = lax.all_to_all(snapshots, "grp", split_axis=1, concat_axis=2, tiled=True)
    panel = jnp.concatenate([scaled, arrived], axis=0).reshape(width, -1)
    local_gram = (
        jnp.dot(panel, panel.T, precision=lax.Precision.HIGHEST, preferred_element_type=jnp.float32)
        / total_cells
    )
    factor = merged_factor(local_gram)
    inverse = lax.linalg.triangular_solve(
        factor, jnp.eye(width, dtype=jnp.float32), left_side=True, lower=True
    )
    result = jnp.dot(
        inverse, panel, precision=lax.Precision.HIGHEST, preferred_element_type=jnp.float32
    )
    result = result.reshape(width, basis_modes.shape[1], basis_modes.shape[2])
    return (result, factor)


def solution(mesh):
    in_specs = (P(None, ("srv", "grp"), None), P(), P(None, "srv", "grp"))
    out_specs = (P(None, ("srv", "grp"), None), P())
    return jax.shard_map(
        per_device, mesh=mesh, in_specs=in_specs, out_specs=out_specs, check_vma=False
    )
```

profile of v0, /device:TPU:0, one launch (start us, length us, event | category | flops | bytes accessed | tf_op | source)
XLA Modules:
  0.0 77.2 jit_solution(11390154502908591722)
XLA Ops:
  0.6 0.0 copy-start
  0.6 0.0 copy-start.1
  0.6 1.2 %copy.19 = f32[16,4,1536]{2,0,1:T(8,128)S(1)} copy(f32[16,4,1536]{2,1,0:T(4,128)} %param.5) | data formatting | bytes 786432 | tf_op args[2]
  1.9 4.0 %all_to_all.18 = f32[16,4,1536]{2,0,1:T(8,128)S(1)} all-to-all(f32[16,4,1536]{2,0,1:T(8,128)S(1)} %copy.19), channel_id=1, replica_groups=mesh['srv'=16,'grp'=2] {'grp'}, dimensions={1} | all-to-all | bytes 786432 | tf_op jit(solution)/shard_map/all_to_all | solution.py:20
  5.9 1.1 %copy.41 = f32[16,2,2,1536]{3,1,0,2:T(2,128)} copy(f32[16,2,2,1536]{3,0,2,1:T(8,128)S(1)} %bitcast.35) | data formatting | bytes 786432 | tf_op jit(solution)/shard_map/all_to_all | solution.py:20
  7.0 0.3 copy.42
  7.3 0.0 copy-done
  7.3 0.0 copy-done.1
  7.3 0.5 copy_multiply_fusion
  7.8 0.5 fusion.17
  8.4 2.1 %all_to_all.16 = f32[16,2,3072]{2,0,1:T(8,128)} reshape(f32[16,2,2,1536]{3,2,0,1:T(2,128)} %bitcast.38) | data formatting | bytes 786432 | tf_op jit(solution)/shard_map/all_to_all | solution.py:20
  10.4 3.4 %fusion.10 = f32[80,80]{0,1:T(8,128)} fusion(f32[16,2,3072]{2,0,1:T(8,128)} %all_to_all.16, f32[64,2,3072]{2,0,1:T(8,128)S(1)} %copy_multiply_fusion), kind=kOutput, calls=%fused_computation.11 | convolution fusion | flops 472357120 | bytes 1991680 | tf_op jit(solution)/shard_map/dot_general | solution.py:23
  13.9 42.4 %psum.7 = f32[80,80]{0,1:T(8,128)S(1)} all-reduce(f32[80,80]{0,1:T(8,128)} %fusion.10), channel_id=1, replica_groups=mesh['srv'=16,'grp'=2] {'srv','grp'}, use_global_device_ids=true, to_apply=%region_0.0 | all-reduce | flops 6400 | bytes 51200 | tf_op jit(solution)/shard_map/psum | solution.py:11
  56.2 0.1 copy.23
  56.3 7.3 %cholesky.17 = f32[80,80]{1,0:T(8,128)S(1)} custom-call(f32[80,80]{1,0:T(8,128)S(1)} %fusion.14), custom_call_target="Cholesky" | custom-call | tf_op jit(solution)/shard_map/jit(cholesky)/cholesky | solution.py:11
  63.7 0.6 compare_reduce_fusion
  64.3 1.3 %select_bitcast_fusion = (f32[1,80,80]{2,1,0:T(8,128)S(1)}, f32[80,80]{1,0:T(8,128)}) fusion(f32[80,80]{1,0:T(8,128)S(1)} %cholesky.17, pred[]{:T(512)} %compare_reduce_fusion), kind=kLoop, calls=%fused_computation.17 | loop fusion | flops 25600 | bytes 76801 | tf_op jit(solution)/shard_map/triangular_solve | solution.py:27
  65.6 6.1 %custom-call.6 = f32[1,80,80]{1,2,0:T(8,128)S(1)} custom-call(f32[1,80,80]{2,1,0:T(8,128)S(1)} %get-tuple-element.8), custom_call_target="InvertDiagBlocksLowerTriangular" | custom-call | tf_op jit(solution)/shard_map/triangular_solve | solution.py:27
  71.7 0.2 convolution_bitcast_fusion
  72.0 0.3 concatenate.12
  72.3 0.1 copy.31
  72.4 0.1 pad_maximum_fusion
  72.6 1.8 %fusion = f32[80,2,3072]{2,0,1:T(8,128)S(1)} fusion(f32[80,80,1]{1,0,2:T(8,128)S(1)} %convolution_bitcast_fusion, f32[10,2,8,3072]{3,2,1,0:T(8,128)S(1)} %bitcast.33), kind=kOutput, calls=%fused_computation | convolution fusion | flops 471859200 | bytes 3957760 | tf_op jit(solution)/shard_map/dot_general | solution.py:30
  74.4 2.8 %copy.26 = f32[80,2,3072]{2,1,0:T(2,128)} copy(f32[80,2,3072]{2,0,1:T(8,128)S(1)} %fusion) | data formatting | bytes 3932160
  (2 shorter events, 0.0 us)
Async XLA Ops:
  0.6 6.7 %copy-start = (f32[64,2,3072]{2,1,0:T(2,128)S(1)}, f32[64,2,3072]{2,1,0:T(2,128)}, u32[]{:S(2)}) copy-start(f32[64,2,3072]{2,1,0:T(2,128)} %param.3) | copy-start | bytes 4718596
  0.6 6.7 %copy-start.1 = (f32[64]{0:T(128)S(1)}, f32[64]{0:T(128)}, u32[]{:S(2)}) copy-start(f32[64]{0:T(128)} %param.4) | copy-start | bytes 772
where the time goes:
time: 77.6 us; the launch traced here: 77.2 us
  blocking collectives  46.4 us (60%)
  other arithmetic  16.6 us (21%)
  local copies, waits for them, and re-layouts  7.98 us (10%)
  matrix products  5.45 us (7%)
    psum x1, blocking collectives, merged_factor(): return jnp.linalg.cholesky(lax.psum(local_gram, ('srv', 'grp')))  42.4 us
    another operation x3, other arithmetic, merged_factor(): return jnp.linalg.cholesky(lax.psum(local_gram, ('srv', 'grp')))  7.98 us
    another operation x2, other arithmetic, per_device(): lax.linalg.triangular_solve(factor, jnp.eye(width, dtype=jnp.float32), le...  7.4 us
    all_to_all x1, blocking collectives, per_device(): lax.all_to_all(snapshots, 'grp', split_axis=1, concat_axis=2, tiled=True)  4.05 us
    unnamed x6, local copies, waits for them, and re-layouts  4.04 us
    all_to_all x3, local copies, waits for them, and re-layouts, per_device(): lax.all_to_all(snapshots, 'grp', split_axis=1, concat_axis=2, tiled=True)  3.43 us
    dot_general x1, matrix products, per_device(): jnp.dot(panel, panel.T, precision=lax.Precision.HIGHEST, preferred_elemen...  3.41 us
    dot_general x1, matrix products, per_device(): jnp.dot(inverse, panel, precision=lax.Precision.HIGHEST, preferred_elemen...  1.82 us

commit v1 on v0

--- a/solution.py
+++ b/solution.py
@@ -7,8 +7,13 @@
 SNAPS = 16
 
 
+def summed_here(shard, name):
+    parts = lax.all_gather(shard, name)
+    return jnp.sum(parts, axis=0)
+
+
 def merged_factor(local_gram):
-    return jnp.linalg.cholesky(lax.psum(local_gram, ("srv", "grp")))
+    return jnp.linalg.cholesky(summed_here(local_gram, ("srv", "grp")))
 
 
 def per_device(basis_modes, weights, snapshots):

time: 77.6 us -> 81.6 us (1.052)
  blocking collectives: 46.4 us -> 51.1 us
    all_gather x0 -> x1, blocking collectives: none -> 47 us  [summed_here(): parts = lax.all_gather(shard, name)]
    psum x1 -> x0, blocking collectives: 42.4 us -> none  [merged_factor(): return jnp.linalg.cholesky(lax.psum(local_gram, ('srv', 'grp')))]
where the time goes in v1:
time: 81.6 us; the launch traced here: 81.3 us
  blocking collectives  51.1 us (63%)
  other arithmetic  16.7 us (20%)
  local copies, waits for them, and re-layouts  7.99 us (10%)
  matrix products  4.83 us (6%)
    all_gather x1, blocking collectives, summed_here(): parts = lax.all_gather(shard, name)  47 us
    another operation x3, other arithmetic, merged_factor(): return jnp.linalg.cholesky(summed_here(local_gram, ('srv', 'grp')))  7.98 us
    another operation x2, other arithmetic, per_device(): lax.linalg.triangular_solve(factor, jnp.eye(width, dtype=jnp.float32), le...  7.4 us
    all_to_all x1, blocking collectives, per_device(): lax.all_to_all(snapshots, 'grp', split_axis=1, concat_axis=2, tiled=True)  4.05 us
    unnamed x6, local copies, waits for them, and re-layouts  4.04 us
    all_to_all x3, local copies, waits for them, and re-layouts, per_device(): lax.all_to_all(snapshots, 'grp', split_axis=1, concat_axis=2, tiled=True)  3.43 us
    dot_general x1, matrix products, per_device(): jnp.dot(panel, panel.T, precision=lax.Precision.HIGHEST, preferred_elemen...  2.79 us
    dot_general x1, matrix products, per_device(): jnp.dot(inverse, panel, precision=lax.Precision.HIGHEST, preferred_elemen...  1.82 us

profile of v1, /device:TPU:0, one launch (start us, length us, event | category | flops | bytes accessed | tf_op | source)
XLA Modules:
  0.0 81.3 jit_solution(8295753857637908935)
XLA Ops:
  0.6 0.0 copy-start
  0.6 0.0 copy-start.1
  0.6 1.2 %copy.17 = f32[16,4,1536]{2,0,1:T(8,128)S(1)} copy(f32[16,4,1536]{2,1,0:T(4,128)} %param.5) | data formatting | bytes 786432 | tf_op args[2]
  1.9 4.0 %all_to_all.18 = f32[16,4,1536]{2,0,1:T(8,128)S(1)} all-to-all(f32[16,4,1536]{2,0,1:T(8,128)S(1)} %copy.17), channel_id=1, replica_groups=mesh['srv'=16,'grp'=2] {'grp'}, dimensions={1} | all-to-all | bytes 786432 | tf_op jit(solution)/shard_map/all_to_all | solution.py:25
  5.9 1.1 %copy.36 = f32[16,2,2,1536]{3,1,0,2:T(2,128)} copy(f32[16,2,2,1536]{3,0,2,1:T(8,128)S(1)} %bitcast.37) | data formatting | bytes 786432 | tf_op jit(solution)/shard_map/all_to_all | solution.py:25
  7.0 0.3 copy.37
  7.3 0.0 copy-done
  7.3 0.0 copy-done.1
  7.3 0.5 copy_multiply_fusion
  7.8 0.5 fusion.17
  8.4 2.1 %all_to_all.16 = f32[16,2,3072]{2,0,1:T(8,128)} reshape(f32[16,2,2,1536]{3,2,0,1:T(2,128)} %bitcast.40) | data formatting | bytes 786432 | tf_op jit(solution)/shard_map/all_to_all | solution.py:25
  10.4 2.8 %fusion.10 = f32[80,80]{1,0:T(8,128)S(1)} fusion(f32[16,2,3072]{2,0,1:T(8,128)} %all_to_all.16, f32[64,2,3072]{2,0,1:T(8,128)S(1)} %copy_multiply_fusion), kind=kOutput, calls=%fused_computation.11 | convolution fusion | flops 472357120 | bytes 1991680 | tf_op jit(solution)/shard_map/dot_general | solution.py:28
  13.2 47.0 %all-gather = f32[2560,80]{1,0:T(8,128)S(1)} all-gather(f32[80,80]{1,0:T(8,128)S(1)} %fusion.10), channel_id=2, replica_groups=mesh['srv'=16,'grp'=2] {'srv','grp'}, dimensions={0}, use_global_device_ids=true | all-gather | bytes 844800 | tf_op jit(solution)/shard_map/all_gather | solution.py:11
  60.3 0.1 reduce_sum.9
  60.4 0.1 copy.20
  60.5 7.3 %cholesky.17 = f32[80,80]{1,0:T(8,128)S(1)} custom-call(f32[80,80]{1,0:T(8,128)S(1)} %fusion.14), custom_call_target="Cholesky" | custom-call | tf_op jit(solution)/shard_map/jit(cholesky)/cholesky | solution.py:16
  67.8 0.6 compare_reduce_fusion
  68.5 1.3 %select_bitcast_fusion = (f32[1,80,80]{2,1,0:T(8,128)S(1)}, f32[80,80]{1,0:T(8,128)}) fusion(f32[80,80]{1,0:T(8,128)S(1)} %cholesky.17, pred[]{:T(512)} %compare_reduce_fusion), kind=kLoop, calls=%fused_computation.17 | loop fusion | flops 25600 | bytes 76801 | tf_op jit(solution)/shard_map/triangular_solve | solution.py:32
  69.7 6.1 %custom-call.6 = f32[1,80,80]{1,2,0:T(8,128)S(1)} custom-call(f32[1,80,80]{2,1,0:T(8,128)S(1)} %get-tuple-element.8), custom_call_target="InvertDiagBlocksLowerTriangular" | custom-call | tf_op jit(solution)/shard_map/triangular_solve | solution.py:32
  75.9 0.2 convolution_bitcast_fusion
  76.1 0.3 concatenate.12
  76.4 0.1 copy.26
  76.5 0.1 pad_maximum_fusion
  76.7 1.8 %fusion = f32[80,2,3072]{2,0,1:T(8,128)S(1)} fusion(f32[80,80,1]{1,0,2:T(8,128)S(1)} %convolution_bitcast_fusion, f32[10,2,8,3072]{3,2,1,0:T(8,128)S(1)} %bitcast.34), kind=kOutput, calls=%fused_computation | convolution fusion | flops 471859200 | bytes 3957760 | tf_op jit(solution)/shard_map/dot_general | solution.py:35
  78.5 2.8 %copy.23 = f32[80,2,3072]{2,1,0:T(2,128)} copy(f32[80,2,3072]{2,0,1:T(8,128)S(1)} %fusion) | data formatting | bytes 3932160
  (2 shorter events, 0.0 us)
Async XLA Ops:
  0.6 6.7 %copy-start = (f32[64,2,3072]{2,1,0:T(2,128)S(1)}, f32[64,2,3072]{2,1,0:T(2,128)}, u32[]{:S(2)}) copy-start(f32[64,2,3072]{2,1,0:T(2,128)} %param.3) | copy-start | bytes 4718596
  0.6 6.7 %copy-start.1 = (f32[64]{0:T(128)S(1)}, f32[64]{0:T(128)}, u32[]{:S(2)}) copy-start(f32[64]{0:T(128)} %param.4) | copy-start | bytes 772

commit v2 on v0

--- a/solution.py
+++ b/solution.py
@@ -8,7 +8,10 @@
 
 
 def merged_factor(local_gram):
-    return jnp.linalg.cholesky(lax.psum(local_gram, ("srv", "grp")))
+    _change_regions = lambda u_in: jax.lax.psum(
+        jax.lax.psum(u_in, axis_name="srv"), axis_name="grp"
+    )
+    return jnp.linalg.cholesky(_change_regions(local_gram))
 
 
 def per_device(basis_modes, weights, snapshots):

time: 77.6 us -> 118 us (1.52)
  blocking collectives: 46.4 us -> 86.8 us
    psum x1 -> x2, blocking collectives: 42.4 us -> 82.7 us  [the longest x1 79.3 us: merged_factor(): jax.lax.psum(u_in, axis_name='srv')]
where the time goes in v2:
time: 118 us
  blocking collectives  86.8 us (74%)
  other arithmetic  16.6 us (14%)
  local copies, waits for them, and re-layouts  7.98 us (7%)
  matrix products  5.45 us (5%)
    psum x1, blocking collectives, merged_factor(): jax.lax.psum(u_in, axis_name='srv')  79.3 us
    another operation x3, other arithmetic, merged_factor(): return jnp.linalg.cholesky(_change_regions(local_gram))  7.98 us
    another operation x2, other arithmetic, per_device(): lax.linalg.triangular_solve(factor, jnp.eye(width, dtype=jnp.float32), le...  7.4 us
    all_to_all x1, blocking collectives, per_device(): lax.all_to_all(snapshots, 'grp', split_axis=1, concat_axis=2, tiled=True)  4.05 us
    unnamed x6, local copies, waits for them, and re-layouts  4.04 us
    psum x1, blocking collectives, merged_factor(): jax.lax.psum(jax.lax.psum(u_in, axis_name='srv'), axis_name='grp')  3.46 us
    all_to_all x3, local copies, waits for them, and re-layouts, per_device(): lax.all_to_all(snapshots, 'grp', split_axis=1, concat_axis=2, tiled=True)  3.43 us
    dot_general x1, matrix products, per_device(): jnp.dot(panel, panel.T, precision=lax.Precision.HIGHEST, preferred_elemen...  3.41 us

profile of v2, /device:TPU:0, one launch (start us, length us, event | category | flops | bytes accessed | tf_op | source)
XLA Modules:
  0.0 117.5 jit_solution(6581803728543397810)
XLA Ops:
  0.6 0.0 copy-start
  0.6 0.0 copy-start.1
  0.6 1.2 %copy.19 = f32[16,4,1536]{2,0,1:T(8,128)S(1)} copy(f32[16,4,1536]{2,1,0:T(4,128)} %param.5) | data formatting | bytes 786432 | tf_op args[2]
  1.9 4.0 %all_to_all.18 = f32[16,4,1536]{2,0,1:T(8,128)S(1)} all-to-all(f32[16,4,1536]{2,0,1:T(8,128)S(1)} %copy.19), channel_id=1, replica_groups=mesh['srv'=16,'grp'=2] {'grp'}, dimensions={1} | all-to-all | bytes 786432 | tf_op jit(solution)/shard_map/all_to_all | solution.py:23
  5.9 1.1 copy.41
  7.0 0.3 copy.42
  7.3 0.0 copy-done
  7.3 0.0 copy-done.1
  7.3 0.5 copy_multiply_fusion
  7.8 0.5 fusion.17
  8.4 2.1 %all_to_all.16 = f32[16,2,3072]{2,0,1:T(8,128)} reshape(f32[16,2,2,1536]{3,2,0,1:T(2,128)} %bitcast.38) | data formatting | bytes 786432 | tf_op jit(solution)/shard_map/all_to_all | solution.py:23
  10.4 3.4 %fusion.10 = f32[80,80]{0,1:T(8,128)} fusion(f32[16,2,3072]{2,0,1:T(8,128)} %all_to_all.16, f32[64,2,3072]{2,0,1:T(8,128)S(1)} %copy_multiply_fusion), kind=kOutput, calls=%fused_computation.11 | convolution fusion | flops 472357120 | bytes 1991680 | tf_op jit(solution)/shard_map/dot_general | solution.py:26
  13.9 79.3 %psum.14 = f32[80,80]{0,1:T(8,128)S(1)} all-reduce(f32[80,80]{0,1:T(8,128)} %fusion.10), channel_id=1, replica_groups=mesh['srv'=16,'grp'=2] {'srv'}, use_global_device_ids=true, to_apply=%region_0.0 | all-reduce | flops 6400 | bytes 51200 | tf_op jit(solution)/shard_map/psum | solution.py:12
  93.1 3.5 %psum.15 = f32[80,80]{0,1:T(8,128)S(1)} all-reduce(f32[80,80]{0,1:T(8,128)S(1)} %psum.14), channel_id=1, replica_groups=mesh['srv'=16,'grp'=2] {'grp'}, use_global_device_ids=true, to_apply=%region_1.0 | all-reduce | flops 6400 | bytes 51200 | tf_op jit(solution)/shard_map/psum | solution.py:11
  96.6 0.1 copy.23
  96.7 7.3 %cholesky.17 = f32[80,80]{1,0:T(8,128)S(1)} custom-call(f32[80,80]{1,0:T(8,128)S(1)} %fusion.14), custom_call_target="Cholesky" | custom-call | tf_op jit(solution)/shard_map/jit(cholesky)/cholesky | solution.py:14
  104.0 0.6 compare_reduce_fusion
  104.7 1.3 %select_bitcast_fusion = (f32[1,80,80]{2,1,0:T(8,128)S(1)}, f32[80,80]{1,0:T(8,128)}) fusion(f32[80,80]{1,0:T(8,128)S(1)} %cholesky.17, pred[]{:T(512)} %compare_reduce_fusion), kind=kLoop, calls=%fused_computation.17 | loop fusion | flops 25600 | bytes 76801 | tf_op jit(solution)/shard_map/triangular_solve | solution.py:30
  105.9 6.1 %custom-call.6 = f32[1,80,80]{1,2,0:T(8,128)S(1)} custom-call(f32[1,80,80]{2,1,0:T(8,128)S(1)} %get-tuple-element.8), custom_call_target="InvertDiagBlocksLowerTriangular" | custom-call | tf_op jit(solution)/shard_map/triangular_solve | solution.py:30
  112.1 0.2 convolution_bitcast_fusion
  112.3 0.3 concatenate.12
  112.7 0.1 copy.31
  112.8 0.1 pad_maximum_fusion
  112.9 1.8 %fusion = f32[80,2,3072]{2,0,1:T(8,128)S(1)} fusion(f32[80,80,1]{1,0,2:T(8,128)S(1)} %convolution_bitcast_fusion, f32[10,2,8,3072]{3,2,1,0:T(8,128)S(1)} %bitcast.33), kind=kOutput, calls=%fused_computation | convolution fusion | flops 471859200 | bytes 3957760 | tf_op jit(solution)/shard_map/dot_general | solution.py:33
  114.7 2.8 %copy.26 = f32[80,2,3072]{2,1,0:T(2,128)} copy(f32[80,2,3072]{2,0,1:T(8,128)S(1)} %fusion) | data formatting | bytes 3932160
  (2 shorter events, 0.0 us)
Async XLA Ops:
  0.6 6.7 %copy-start = (f32[64,2,3072]{2,1,0:T(2,128)S(1)}, f32[64,2,3072]{2,1,0:T(2,128)}, u32[]{:S(2)}) copy-start(f32[64,2,3072]{2,1,0:T(2,128)} %param.3) | copy-start | bytes 4718596
  0.6 6.7 %copy-start.1 = (f32[64]{0:T(128)S(1)}, f32[64]{0:T(128)}, u32[]{:S(2)}) copy-start(f32[64]{0:T(128)} %param.4) | copy-start | bytes 772
